TPU v7x, 32 devices: a whole 2x2x4 slice. The times are simulated.
32 devices in a mesh: band: 8 (over z, x), space: 4 (over y, core).
Axes of the slice: x: 2, y: 2, z: 4, core: 2. Of those that a mesh axis runs over, the one named last changes fastest.
Arguments:
- orbitals: bfloat16 [64, 64, 160, 128], P('band', None, 'space'), may hold values from -8.5 to 8.5
- occupations: float32 [64], P('band'), may hold values from 0.07 to 2.5
Outputs:
- potential: float32 [64, 160, 128], P('band', 'space')
All inputs are finite; a program needn't handle non-finite values.
Results may differ from a plain program's by a relative error of at most 0.0003.
Values sent between devices are 32-bit elements; how exact they have to be, the bound alone decides.
A program may use at most 64 MiB of HBM per device.

v0:
```python
import math

import jax
import jax.numpy as jnp
from jax import lax
from jax.sharding import PartitionSpec as P

ITERS = 3


four_pi = 4.0 * math.pi


def with_halo(shard, sides, width):
    for axis, dim in sides:
        peers, length = (lax.axis_size(axis), shard.shape[dim])
        up = [(i, (i + 1) % peers) for i in range(peers - 1)]
        down = [(j, i) for i, j in up]
        last = lax.slice_in_dim(shard, length - width, length, axis=dim)
        first = lax.slice_in_dim(shard, 0, width, axis=dim)
        before = lax.ppermute(last, axis, up)
        after = lax.ppermute(first, axis, down)
        shard = jnp.concatenate([before, shard, after], axis=dim)
    return shard


def stencil(padded):
    center = padded[2:-2, 2:-2, 2:-2]
    near = padded[3:-1, 2:-2, 2:-2] + padded[1:-3, 2:-2, 2:-2]
    near = near + padded[2:-2, 3:-1, 2:-2] + padded[2:-2, 1:-3, 2:-2]
    near = near + padded[2:-2, 2:-2, 3:-1] + padded[2:-2, 2:-2, 1:-3]
    distant = padded[4:, 2:-2, 2:-2] + padded[:-4, 2:-2, 2:-2]
    distant = distant + padded[2:-2, 4:, 2:-2] + padded[2:-2, :-4, 2:-2]
    distant = distant + padded[2:-2, 2:-2, 4:] + padded[2:-2, 2:-2, :-4]
    return 7.5 * center - 4.0 / 3.0 * near + 1.0 / 12.0 * distant


def operate(field):
    widened = with_halo(field, (("band", 0), ("space", 1)), 2)
    return stencil(jnp.pad(widened, ((0, 0), (0, 0), (2, 2))))


def paired_sums(residual, image):
    return lax.psum((jnp.sum(residual * residual), jnp.sum(residual * image)), ("band", "space"))


def local(orbitals, occupations):

    def accumulate(index, total):
        wave = lax.dynamic_index_in_dim(orbitals, index, 0, keepdims=False).astype(jnp.float32)
        return total + occupations[index] * wave * wave

    start = jnp.zeros(orbitals.shape[1:], jnp.float32)
    partial_value = lax.fori_loop(0, orbitals.shape[0], accumulate, start)
    groups = lax.axis_size("band")
    summed = lax.psum(partial_value, "band")
    share = orbitals.shape[1] // groups
    mine = lax.dynamic_slice_in_dim(summed, lax.axis_index("band") * share, share, 0)
    density = mine / (orbitals.shape[0] * groups)
    source = four_pi * density
    potential = jnp.zeros_like(source)
    residual = source
    image = operate(residual)
    norm_now, product = paired_sums(residual, image)
    alpha = norm_now / product
    direction, along = (residual, image)
    for step in range(ITERS):
        potential = potential + alpha * direction
        residual = residual - alpha * along
        if step + 1 < ITERS:
            image = operate(residual)
            norm_next, product = paired_sums(residual, image)
            ratio = norm_next / norm_now
            alpha = norm_next / (product - ratio * norm_next / alpha)
            direction = residual + ratio * direction
            along = image + ratio * along
            norm_now = norm_next
    return potential


def solution(mesh):
    in_specs = (P("band", None, "space", None), P("band"))
    out_specs = P("band", "space", None)
    return jax.shard_map(local, mesh=mesh, in_specs=in_specs, out_specs=out_specs, check_vma=False)
```

profile of v0, /device:TPU:0, one launch (start us, length us, event | category | flops | bytes accessed | tf_op | source)
XLA Modules:
  0.0 320.6 jit_solution(14691085561565989361)
XLA Ops:
  6.5 30.2 %while.14 = (s32[]{:T(128)}, f32[64,40,128]{2,1,0:T(8,128)S(1)}, f32[8]{0:T(128)}, bf16[8,64,40,128]{3,2,1,0:T(8,128)(2,1)}, s32[]{:T(128)}, /*index=5*/s32[]{:T(128)}) while((s32[]{:T(128)}, f32[64,40,128]{2,1,0:T(8,128)S(1)}, f32[8]{0:T(128)}, bf16[8,64,40,128]{3,2,1,0:T(8,128)(2,1)}, s32[]{:T(128)}, /*index=5*/s32[]{:T(128)}) %tuple.46), condition=%wide.region_1.2_spmd.clone, body=%wide.region_0.1_spmd.clone.sunk | while | flops 1638403 | bytes 3276907 | solution.py:54
  6.5 1.3 dynamic_slice.31
  7.8 2.5 fusion.46
  10.3 1.3 dynamic_slice.31
  11.6 2.5 fusion.46
  14.1 1.3 dynamic_slice.31
  15.4 2.5 fusion.46
  17.9 1.3 dynamic_slice.31
  19.2 2.5 fusion.46
  21.6 1.3 dynamic_slice.31
  22.9 2.5 fusion.46
  25.4 1.3 dynamic_slice.31
  26.7 2.5 fusion.46
  29.2 1.3 dynamic_slice.31
  30.5 2.5 fusion.46
  33.0 1.3 dynamic_slice.31
  34.3 2.5 fusion.46
  36.8 1.1 copy-done
  37.9 86.5 %all-reduce.8.cloned.1.call-done = f32[64,40,128]{2,1,0:T(8,128)} async-done(((f32[64,40,128]{2,1,0:T(8,128)}), f32[64,40,128]{2,1,0:T(8,128)}) %all-reduce.8.cloned.1.call-update) | async-done | bytes 1310736 | tf_op jit(solution)/shard_map/psum | solution.py:56
  124.4 0.9 dynamic-slice_multiply_fusion
  125.3 3.4 %collective-permute-start.1 = (f32[2,40,128]{2,1,0:T(8,128)S(1)}, f32[2,40,128]{2,1,0:T(8,128)S(1)}, u32[]{:S(2)}, u32[]{:S(2)}) collective-permute-start(f32[2,40,128]{2,1,0:T(8,128)S(1)} %get-tuple-element.138), channel_id=1, source_target_pairs={{0,4},{4,8},{8,12},{12,16},{16,20},{20,24},{24,28},{1,5},{5,9},{9,... | collective-permute-start | bytes 122888 | tf_op jit(solution)/shard_map/ppermute | solution.py:21
  128.7 1.3 collective-permute-start
  130.0 0.4 collective-permute-done.1
  130.3 4.2 %collective-permute-done = f32[2,40,128]{2,1,0:T(8,128)S(1)} collective-permute-done((f32[2,40,128]{2,1,0:T(8,128)S(1)}, f32[2,40,128]{2,1,0:T(8,128)S(1)}, u32[]{:S(2)}, u32[]{:S(2)}) %collective-permute-start) | collective-permute-done | bytes 40992 | tf_op jit(solution)/shard_map/ppermute | solution.py:22
  134.6 1.3 collective-permute-start.3
  135.9 1.3 collective-permute-start.2
  137.2 3.5 %collective-permute-done.2 = f32[12,2,128]{2,1,0:T(2,128)S(1)} collective-permute-done((f32[12,2,128]{2,1,0:T(2,128)S(1)}, f32[12,2,128]{2,1,0:T(2,128)S(1)}, u32[]{:S(2)}, u32[]{:S(2)}) %collective-permute-start.2) | collective-permute-done | bytes 12320 | tf_op jit(solution)/shard_map/ppermute | solution.py:22
  141.0 1.8 multiply_reduce_fusion.3
  142.8 41.2 %all-reduce.5 = (f32[]{:T(128)}, f32[]{:T(128)}) all-reduce(f32[]{:T(128)} %get-tuple-element.105, f32[]{:T(128)} %get-tuple-element.104), channel_id=1, replica_groups=mesh['band'=8,'space'=4] {'band','space'}, use_global_device_ids=true, to_apply=%region_4.5 | all-reduce | flops 2 | bytes 16 | tf_op jit(solution)/shard_map/psum | solution.py:44
  185.3 0.9 multiply_subtract_fusion.1
  186.3 4.2 %collective-permute-start.5 = (f32[2,40,128]{2,1,0:T(8,128)S(1)}, f32[2,40,128]{2,1,0:T(8,128)S(1)}, u32[]{:S(2)}, u32[]{:S(2)}) collective-permute-start(f32[2,40,128]{2,1,0:T(8,128)S(1)} %get-tuple-element.136), channel_id=1, source_target_pairs={{0,4},{4,8},{8,12},{12,16},{16,20},{20,24},{24,28},{1,5},{5,9},{9,... | collective-permute-start | bytes 122888 | tf_op jit(solution)/shard_map/ppermute | solution.py:21
  190.5 1.3 collective-permute-start.4
  191.8 0.4 collective-permute-done.5
  192.1 4.2 %collective-permute-done.4 = f32[2,40,128]{2,1,0:T(8,128)S(1)} collective-permute-done((f32[2,40,128]{2,1,0:T(8,128)S(1)}, f32[2,40,128]{2,1,0:T(8,128)S(1)}, u32[]{:S(2)}, u32[]{:S(2)}) %collective-permute-start.4) | collective-permute-done | bytes 40992 | tf_op jit(solution)/shard_map/ppermute | solution.py:22
  196.4 1.3 collective-permute-start.7
  197.7 1.3 collective-permute-start.6
  199.0 2.8 collective-permute-done.6
  202.1 0.9 multiply_reduce_fusion.1
  203.0 41.9 %all-reduce.4 = (f32[]{:T(128)}, f32[]{:T(128)}) all-reduce(f32[]{:T(128)} %get-tuple-element.103, f32[]{:T(128)} %get-tuple-element.102), channel_id=1, replica_groups=mesh['band'=8,'space'=4] {'band','space'}, use_global_device_ids=true, to_apply=%region_8.9 | all-reduce | flops 2 | bytes 16 | tf_op jit(solution)/shard_map/psum | solution.py:44
  249.4 4.2 %collective-permute-start.9 = (f32[2,40,128]{2,1,0:T(8,128)S(1)}, f32[2,40,128]{2,1,0:T(8,128)S(1)}, u32[]{:S(2)}, u32[]{:S(2)}) collective-permute-start(f32[2,40,128]{2,1,0:T(8,128)S(1)} %get-tuple-element.134), channel_id=1, source_target_pairs={{0,4},{4,8},{8,12},{12,16},{16,20},{20,24},{24,28},{1,5},{5,9},{9,... | collective-permute-start | bytes 122888 | tf_op jit(solution)/shard_map/ppermute | solution.py:21
  253.6 1.3 collective-permute-start.8
  255.2 4.2 %collective-permute-done.8 = f32[2,40,128]{2,1,0:T(8,128)S(1)} collective-permute-done((f32[2,40,128]{2,1,0:T(8,128)S(1)}, f32[2,40,128]{2,1,0:T(8,128)S(1)}, u32[]{:S(2)}, u32[]{:S(2)}) %collective-permute-start.8) | collective-permute-done | bytes 40992 | tf_op jit(solution)/shard_map/ppermute | solution.py:22
  259.5 1.3 collective-permute-start.11
  260.8 1.3 collective-permute-start.10
  262.1 3.1 collective-permute-done.10
  265.6 0.9 fusion.39
  266.5 41.9 %all-reduce.3 = (f32[]{:T(128)}, f32[]{:T(128)}) all-reduce(f32[]{:T(128)} %get-tuple-element.101, f32[]{:T(128)} %get-tuple-element.100), channel_id=1, replica_groups=mesh['band'=8,'space'=4] {'band','space'}, use_global_device_ids=true, to_apply=%region_12.13 | all-reduce | flops 2 | bytes 16 | tf_op jit(solution)/shard_map/psum | solution.py:44
  312.1 1.6 multiply_add_fusion
  (21 shorter events, 1.4 us)
Async XLA Ops:
  6.5 117.8 %all-reduce.8.cloned.1.call-start = ((), (), s32[]{:S(2)}) async-start(), calls=%async_computation | async-start | bytes 2621440 | tf_op jit(solution)/shard_map/psum | solution.py:56
  36.7 1.1 copy-start
  125.3 5.0 %collective-permute-start.1 = (f32[2,40,128]{2,1,0:T(8,128)S(1)}, f32[2,40,128]{2,1,0:T(8,128)S(1)}, u32[]{:S(2)}, u32[]{:S(2)}) collective-permute-start(f32[2,40,128]{2,1,0:T(8,128)S(1)} %get-tuple-element.138), channel_id=1, source_target_pairs={{0,4},{4,8},{8,12},{12,16},{16,20},{20,24},{24,28},{1,5},{5,9},{9,... | collective-permute-start | bytes 122888 | tf_op jit(solution)/shard_map/ppermute | solution.py:21
  128.7 5.9 %collective-permute-start = (f32[2,40,128]{2,1,0:T(8,128)S(1)}, f32[2,40,128]{2,1,0:T(8,128)S(1)}, u32[]{:S(2)}, u32[]{:S(2)}) collective-permute-start(f32[2,40,128]{2,1,0:T(8,128)S(1)} %get-tuple-element.139), channel_id=1, source_target_pairs={{4,0},{8,4},{12,8},{16,12},{20,16},{24,20},{28,24},{5,1},{9,5},{13... | collective-permute-start | bytes 122888 | tf_op jit(solution)/shard_map/ppermute | solution.py:22
  134.6 2.6 collective-permute-start.3
  135.9 4.8 %collective-permute-start.2 = (f32[12,2,128]{2,1,0:T(2,128)S(1)}, f32[12,2,128]{2,1,0:T(2,128)S(1)}, u32[]{:S(2)}, u32[]{:S(2)}) collective-permute-start(f32[12,2,128]{2,1,0:T(2,128)S(1)} %get-tuple-element.133), channel_id=1, source_target_pairs={{1,0},{2,1},{3,2},{5,4},{6,5},{7,6},{9,8},{10,9},{11,10},{13,12},{... | collective-permute-start | bytes 36872 | tf_op jit(solution)/shard_map/ppermute | solution.py:22
  186.3 5.8 %collective-permute-start.5 = (f32[2,40,128]{2,1,0:T(8,128)S(1)}, f32[2,40,128]{2,1,0:T(8,128)S(1)}, u32[]{:S(2)}, u32[]{:S(2)}) collective-permute-start(f32[2,40,128]{2,1,0:T(8,128)S(1)} %get-tuple-element.136), channel_id=1, source_target_pairs={{0,4},{4,8},{8,12},{12,16},{16,20},{20,24},{24,28},{1,5},{5,9},{9,... | collective-permute-start | bytes 122888 | tf_op jit(solution)/shard_map/ppermute | solution.py:21
  190.5 5.9 %collective-permute-start.4 = (f32[2,40,128]{2,1,0:T(8,128)S(1)}, f32[2,40,128]{2,1,0:T(8,128)S(1)}, u32[]{:S(2)}, u32[]{:S(2)}) collective-permute-start(f32[2,40,128]{2,1,0:T(8,128)S(1)} %get-tuple-element.137), channel_id=1, source_target_pairs={{4,0},{8,4},{12,8},{16,12},{20,16},{24,20},{28,24},{5,1},{9,5},{13... | collective-permute-start | bytes 122888 | tf_op jit(solution)/shard_map/ppermute | solution.py:22
  196.4 2.6 collective-permute-start.7
  197.7 4.1 %collective-permute-start.6 = (f32[12,2,128]{2,1,0:T(2,128)S(1)}, f32[12,2,128]{2,1,0:T(2,128)S(1)}, u32[]{:S(2)}, u32[]{:S(2)}) collective-permute-start(f32[12,2,128]{2,1,0:T(2,128)S(1)} %get-tuple-element.129), channel_id=1, source_target_pairs={{1,0},{2,1},{3,2},{5,4},{6,5},{7,6},{9,8},{10,9},{11,10},{13,12},{... | collective-permute-start | bytes 36872 | tf_op jit(solution)/shard_map/ppermute | solution.py:22
  249.4 5.8 %collective-permute-start.9 = (f32[2,40,128]{2,1,0:T(8,128)S(1)}, f32[2,40,128]{2,1,0:T(8,128)S(1)}, u32[]{:S(2)}, u32[]{:S(2)}) collective-permute-start(f32[2,40,128]{2,1,0:T(8,128)S(1)} %get-tuple-element.134), channel_id=1, source_target_pairs={{0,4},{4,8},{8,12},{12,16},{16,20},{20,24},{24,28},{1,5},{5,9},{9,... | collective-permute-start | bytes 122888 | tf_op jit(solution)/shard_map/ppermute | solution.py:21
  253.6 5.9 %collective-permute-start.8 = (f32[2,40,128]{2,1,0:T(8,128)S(1)}, f32[2,40,128]{2,1,0:T(8,128)S(1)}, u32[]{:S(2)}, u32[]{:S(2)}) collective-permute-start(f32[2,40,128]{2,1,0:T(8,128)S(1)} %get-tuple-element.135), channel_id=1, source_target_pairs={{4,0},{8,4},{12,8},{16,12},{20,16},{24,20},{28,24},{5,1},{9,5},{13... | collective-permute-start | bytes 122888 | tf_op jit(solution)/shard_map/ppermute | solution.py:22
  259.5 2.6 collective-permute-start.11
  260.8 4.4 %collective-permute-start.10 = (f32[12,2,128]{2,1,0:T(2,128)S(1)}, f32[12,2,128]{2,1,0:T(2,128)S(1)}, u32[]{:S(2)}, u32[]{:S(2)}) collective-permute-start(f32[12,2,128]{2,1,0:T(2,128)S(1)} %get-tuple-element.125), channel_id=1, source_target_pairs={{1,0},{2,1},{3,2},{5,4},{6,5},{7,6},{9,8},{10,9},{11,10},{13,12},{... | collective-permute-start | bytes 36872 | tf_op jit(solution)/shard_map/ppermute | solution.py:22
Sparse Core Ops, SparseCore 0:
  38.0 86.3 all-reduce.7
where the time goes:
time: 322 us; the launch traced here: 321 us
  blocking collectives  125 us (39%)
  waiting for transfers between devices  110 us (34%)
  other arithmetic  27.8 us (9%)
  starting transfers between devices  23.4 us (7%)
  between operations  23 us (7%)
  local copies, waits for them, and re-layouts  11.5 us (4%)
    psum x3, blocking collectives, paired_sums(): lax.psum((jnp.sum(residual * residual), jnp.sum(residual * image)), ('ban...  125 us
    psum x1, waiting for transfers between devices, local(): summed = lax.psum(partial_value, 'band')  86.5 us
    ppermute x6, waiting for transfers between devices, with_halo(): after = lax.ppermute(first, axis, down)  22.1 us
    add x8, other arithmetic, accumulate(): return total + occupations[index] * wave * wave  19.6 us
    ppermute x6, starting transfers between devices, with_halo(): before = lax.ppermute(last, axis, up)  15.6 us
    dynamic_slice x8, local copies, waits for them, and re-layouts, accumulate(): return total + occupations[index] * wave * wave  10.4 us
    ppermute x6, starting transfers between devices, with_halo(): after = lax.ppermute(first, axis, down)  7.75 us
  transfers between devices with their start and end apart: 13, of which 10 were waited for; matrix products, arithmetic and copies ran while one was open for 0% of the time, Pallas kernels for 0%

commit v1 on v0

v1 whole, which is shorter than its diff:
```python
import functools
import math

import jax
import jax.numpy as jnp
from jax import lax
from jax.experimental import pallas as pl
from jax.experimental.pallas import tpu as pltpu
from jax.sharding import PartitionSpec as P

MESH = pl.DeviceIdType.MESH
REACH = 2
DEEP = 3 * REACH
EDGE = 8
CORNER = 2 * REACH
DIRECTIONS = ((1, 0), (-1, 0), (0, 1), (0, -1), (1, 1), (1, -1), (-1, 1), (-1, -1))


def permuted(position, order, stages):
    offset = 0
    for s, bit in enumerate(order):
        digit = (position // (1 << (stages - 1 - s))) % 2
        offset = offset + digit * (1 << bit)
    return offset


def flipped(index, offset, stages):
    total = 0
    for k in range(stages):
        a, b = (index // (1 << k)) % 2, (offset // (1 << k)) % 2
        total = total + ((a + b) % 2) * (1 << k)
    return total


def kernel(bands, spaces, groups, bands_total, chunks, orders, occ_ref, orb_ref, out_ref,
           held, acc, got, field, first, second, mine, theirs, band_sum, space_sums,
           load_sem, rs_send, rs_recv, halo_send, halo_recv, mb_send, mb_recv, ms_send, ms_recv):
    b, s = lax.axis_index("band"), lax.axis_index("space")
    stages = len(orders[0])
    planes, rows, lanes = out_ref.shape
    part = planes // chunks
    tall = rows + 2 * EDGE

    loads = {}
    for q in range(bands - 1, -1, -1):
        share = flipped(b, q, stages)
        loads[q] = pltpu.make_async_copy(
            orb_ref.at[:, pl.ds(share * planes, planes)], held.at[q], load_sem.at[q])
        loads[q].start()

    field[...] = jnp.zeros_like(field)

    barrier = pltpu.get_barrier_semaphore()
    greet = [((b + k) % bands, s) for k in range(1, bands)]
    greet += [(b, (s + k) % spaces) for k in range(1, spaces)]
    greet += [((b + db + bands) % bands, (s + ds + spaces) % spaces)
              for db, ds in DIRECTIONS if db and ds]
    for peer in greet:
        pl.semaphore_signal(barrier, inc=1, device_id=peer, device_id_type=MESH)

    for q in range(bands):
        loads[q].wait()

    weights = [occ_ref[k] for k in range(groups)]

    def density(c, low, high):
        def body(i, _):
            position = low + i // part
            plane = i % part
            offset = permuted(position, orders[c], stages)
            total = jnp.zeros((rows, lanes), jnp.float32)
            for k in range(groups):
                wave = held[offset, k, c * part + plane].astype(jnp.float32)
                total = total + (weights[k] * wave) * wave
            acc[c, position, plane] = total
            return 0
        lax.fori_loop(0, (high - low) * part, body, 0)

    def hop(c, stage):
        half = bands >> (stage + 1)
        bit = 1 << orders[c][stage]
        peer = b + bit * (1 - 2 * ((b // bit) % 2))
        return pltpu.make_async_remote_copy(
            src_ref=acc.at[c, pl.ds(half, half)], dst_ref=got.at[c, pl.ds(half, half)],
            send_sem=rs_send.at[c, stage], recv_sem=rs_recv.at[c, stage],
            device_id=(peer, s), device_id_type=MESH)

    hops = {(c, t): hop(c, t) for c in range(chunks) for t in range(stages)}
    for c in range(chunks):
        density(c, bands // 2, bands)
        if c == 0:
            pl.semaphore_wait(barrier, len(greet))
        hops[c, 0].start()
    for c in range(chunks):
        density(c, 0, bands // 2)

    scale = 4.0 * math.pi / bands_total
    order = sorted(hops, key=lambda ct: (ct[0] // 2 + ct[1], -ct[1], ct[0]))
    for c, t in order:
        half = bands >> (t + 1)
        hops[c, t].wait_recv()

        if t + 1 < stages:
            quarter = half // 2

            def add(i, _):
                position, plane = i // part, i % part
                acc[c, position, plane] = acc[c, position, plane] + got[c, half + position, plane]
                return 0
            lax.fori_loop(quarter * part, half * part, add, 0)
            hops[c, t + 1].start()
            lax.fori_loop(0, quarter * part, add, 0)
        else:
            for plane in range(part):
                field[DEEP + c * part + plane, EDGE:EDGE + rows] = scale * (
                    acc[c, 0, plane] + got[c, 1, plane])

    def span(d, size, width, halo):
        if d > 0:
            return size + halo - width, halo - width
        return halo, size + halo

    halos = []
    for i, (db, ds) in enumerate(DIRECTIONS):
        deep = DEEP if not ds else (CORNER if db else planes)
        wide = EDGE if ds else rows
        src_p, dst_p = span(db, planes, deep, DEEP) if db else (DEEP, DEEP)
        src_r, dst_r = span(ds, rows, wide, EDGE) if ds else (EDGE, EDGE)
        to = ((b + db + bands) % bands, (s + ds + spaces) % spaces)
        copy = pltpu.make_async_remote_copy(
            src_ref=field.at[pl.ds(src_p, deep), pl.ds(src_r, wide)],
            dst_ref=field.at[pl.ds(dst_p, deep), pl.ds(dst_r, wide)],
            send_sem=halo_send.at[i], recv_sem=halo_recv.at[i],
            device_id=to, device_id_type=MESH)

        def inside(x, y, db=db, ds=ds):
            ok = None
            for d, v, n in ((db, x, bands), (ds, y, spaces)):
                if d:
                    here = (v + d >= 0) & (v + d < n)
                    ok = here if ok is None else ok & here
            return ok
        sends = inside(b, s)
        takes = None
        for d, v, n in ((db, b, bands), (ds, s, spaces)):
            if d:
                here = (v - d >= 0) & (v - d < n)
                takes = here if takes is None else takes & here
        pl.when(sends)(copy.start)
        halos.append((copy, sends, takes))
    for copy, sends, takes in halos:
        pl.when(takes)(copy.wait_recv)
    for copy, sends, takes in halos:
        pl.when(sends)(copy.wait_send)

    row = lax.broadcasted_iota(jnp.int32, (tall, lanes), 0)
    lane = lax.broadcasted_iota(jnp.int32, (tall, lanes), 1)
    low_row = jnp.where(s == 0, EDGE, 0)
    high_row = jnp.where(s == spaces - 1, EDGE + rows, tall)
    rows_in = ((row >= low_row) & (row < high_row)).astype(jnp.float32)
    near, far = -4.0 / 3.0, 1.0 / 12.0
    lane_terms = [(shift % lanes, jnp.where((lane - shift >= 0) & (lane - shift < lanes), w, 0.0))
                  for shift, w in ((1, near), (-1, near), (2, far), (-2, far))]
    low_plane = jnp.where(b == 0, DEEP, 0)
    high_plane = jnp.where(b == bands - 1, DEEP + planes, planes + 2 * DEEP)

    def apply(ref, p):
        v = ref[p]
        ones = ref[p - 1] + ref[p + 1] + pltpu.roll(v, 1, 0) + pltpu.roll(v, tall - 1, 0)
        twos = ref[p - 2] + ref[p + 2] + pltpu.roll(v, 2, 0) + pltpu.roll(v, tall - 2, 0)
        total = 7.5 * v + near * ones + far * twos
        for shift, coefficient in lane_terms:
            total = total + coefficient * pltpu.roll(v, shift, 1)
        return total

    def step(src, dst):
        def body(p, _):
            here = jnp.where((p >= low_plane) & (p < high_plane), 1.0, 0.0)
            dst[p] = apply(src, p) * (rows_in * here)
            return 0
        return body

    lax.fori_loop(REACH, planes + 2 * DEEP - REACH, step(field, first), 0)
    lax.fori_loop(2 * REACH, planes + 2 * DEEP - 2 * REACH, step(first, second), 0)

    def fold(x):
        x = x[EDGE:EDGE + rows]
        total = x[0:8]
        for k in range(8, rows, 8):
            total = total + x[k:k + 8]
        return total

    def moments(p, sums):
        w0, w1, w2 = field[p], first[p], second[p]
        w3 = apply(second, p)
        terms = (w0 * w0, w0 * w1, w1 * w1, w1 * w2, w2 * w2, w2 * w3)
        return tuple(x + fold(y) for x, y in zip(sums, terms))

    sums = lax.fori_loop(DEEP, DEEP + planes, moments,
                         tuple(jnp.zeros((8, lanes), jnp.float32) for _ in range(6)))
    packed = [jnp.sum(x, axis=0, keepdims=True) for x in sums]
    packed = jnp.concatenate(packed + [jnp.zeros((2, lanes), jnp.float32)], axis=0)
    mine[...] = packed
    copies = []
    for k in range(1, bands):
        copies.append(pltpu.make_async_remote_copy(
            src_ref=mine, dst_ref=theirs.at[b], send_sem=mb_send.at[k], recv_sem=mb_recv.at[k],
            device_id=((b + k) % bands, s), device_id_type=MESH))
        copies[-1].start()
    theirs[b] = packed
    for copy in copies:
        copy.wait_recv()
    total = theirs[0]
    for k in range(1, bands):
        total = total + theirs[k]
    band_sum[...] = total
    across = []
    for k in range(1, spaces):
        across.append(pltpu.make_async_remote_copy(
            src_ref=band_sum, dst_ref=space_sums.at[s], send_sem=ms_send.at[k],
            recv_sem=ms_recv.at[k], device_id=(b, (s + k) % spaces), device_id_type=MESH))
        across[-1].start()
    space_sums[s] = total
    for copy in across:
        copy.wait_recv()
    total = space_sums[0]
    for k in range(1, spaces):
        total = total + space_sums[k]
    total = jnp.sum(total, axis=1, keepdims=True)
    mu = [total[k:k + 1] for k in range(6)]

    def form(c, shift):
        value = None
        for i in range(len(c)):
            for j in range(i, len(c)):
                term = c[i] * c[j] * mu[i + j + shift]
                term = term if i == j else 2.0 * term
                value = term if value is None else value + term
        return value

    alpha0 = mu[0] / mu[1]
    r1 = [jnp.ones_like(alpha0), -alpha0]
    rr1 = form(r1, 0)
    beta0 = rr1 / mu[0]
    d1 = [1.0 + beta0, -alpha0]
    alpha1 = rr1 / form(d1, 1)
    r2 = [r1[0], r1[1] - alpha1 * d1[0], -alpha1 * d1[1]]
    rr2 = form(r2, 0)
    beta1 = rr2 / rr1
    d2 = [r2[0] + beta1 * d1[0], r2[1] + beta1 * d1[1], r2[2]]
    alpha2 = rr2 / form(d2, 1)
    c0 = alpha0 + alpha1 * d1[0] + alpha2 * d2[0]
    c1 = alpha1 * d1[1] + alpha2 * d2[1]
    c2 = alpha2 * d2[2]

    for p in range(planes):
        at = (DEEP + p, slice(EDGE, EDGE + rows))
        out_ref[p] = c0 * field[at] + c1 * first[at] + c2 * second[at]

    for c, t in order:
        hops[c, t].wait_send()
    for copy in copies + across:
        copy.wait_send()


def solution(mesh):
    bands, spaces = mesh.shape["band"], mesh.shape["space"]
    stages = bands.bit_length() - 1

    def local(orbitals, occupations):
        groups, length, rows, lanes = orbitals.shape
        planes = length // bands
        chunks = 4
        part = planes // chunks
        forward = list(range(stages))
        half = stages // 2
        swapped = forward[half:half + 1] + forward[:half] + forward[half + 1:]
        orders = [forward if c % 2 == 0 else swapped for c in range(chunks)]
        body = functools.partial(kernel, bands, spaces, groups, groups * bands, chunks, orders)
        tall, deep = rows + 2 * EDGE, planes + 2 * DEEP
        f32 = jnp.float32
        return pl.pallas_call(
            body,
            out_shape=jax.ShapeDtypeStruct((planes, rows, lanes), f32),
            in_specs=[pl.BlockSpec(memory_space=pltpu.SMEM), pl.BlockSpec(memory_space=pl.ANY)],
            out_specs=pl.BlockSpec(memory_space=pltpu.VMEM),
            scratch_shapes=[
                pltpu.VMEM((bands, groups, planes, rows, lanes), orbitals.dtype),
                pltpu.VMEM((chunks, bands, part, rows, lanes), f32),
                pltpu.VMEM((chunks, bands, part, rows, lanes), f32),
                pltpu.VMEM((deep, tall, lanes), f32),
                pltpu.VMEM((deep, tall, lanes), f32),
                pltpu.VMEM((deep, tall, lanes), f32),
                pltpu.VMEM((8, lanes), f32),
                pltpu.VMEM((bands, 8, lanes), f32),
                pltpu.VMEM((8, lanes), f32),
                pltpu.VMEM((spaces, 8, lanes), f32),
                pltpu.SemaphoreType.DMA((bands,)),
                pltpu.SemaphoreType.DMA((chunks, stages)),
                pltpu.SemaphoreType.DMA((chunks, stages)),
                pltpu.SemaphoreType.DMA((len(DIRECTIONS),)),
                pltpu.SemaphoreType.DMA((len(DIRECTIONS),)),
                pltpu.SemaphoreType.DMA((bands,)),
                pltpu.SemaphoreType.DMA((bands,)),
                pltpu.SemaphoreType.DMA((spaces,)),
                pltpu.SemaphoreType.DMA((spaces,)),
            ],
            compiler_params=pltpu.CompilerParams(
                collective_id=0, has_side_effects=True, vmem_limit_bytes=48 * 1024 * 1024),
        )(occupations, orbitals)

    in_specs = (P("band", None, "space", None), P("band"))
    out_specs = P("band", "space", None)
    return jax.shard_map(local, mesh=mesh, in_specs=in_specs, out_specs=out_specs, check_vma=False)
```

time: 322 us -> 49.2 us (0.15)
  blocking collectives: 125 us -> 0 us
  waiting for transfers between devices: 110 us -> 0 us
  Pallas kernels: 0 us -> 45.3 us
  other arithmetic: 27.8 us -> 0 us
  starting transfers between devices: 23.4 us -> 0 us
  between operations: 23 us -> 0.01 us
  local copies, waits for them, and re-layouts: 11.5 us -> 3.81 us
    psum x3 -> x0, blocking collectives: 125 us -> none  [paired_sums(): lax.psum((jnp.sum(residual * residual), jnp.sum(residual * image)), ('ban...]
    psum x1 -> x0, waiting for transfers between devices: 86.5 us -> none  [local(): summed = lax.psum(partial_value, 'band')]
    pallas_call x0 -> x1, Pallas kernels: none -> 45.3 us  [local(): pl.pallas_call(body, out_shape=jax.ShapeDtypeStruct((planes, rows, lanes)...]
    ppermute x12 -> x0, starting transfers between devices: 23.4 us -> none  [the longest x6 15.6 us: with_halo(): before = lax.ppermute(last, axis, up)]
    ppermute x12 -> x0, waiting for transfers between devices: 23.2 us -> none  [the longest x6 22.1 us: with_halo(): after = lax.ppermute(first, axis, down)]
    add x9 -> x0, other arithmetic: 21.2 us -> none  [the longest x8 19.6 us: accumulate(): return total + occupations[index] * wave * wave]
    dynamic_slice x8 -> x0, local copies, waits for them, and re-layouts: 10.4 us -> none  [accumulate(): return total + occupations[index] * wave * wave]
    reduce_sum x3 -> x0, other arithmetic: 3.63 us -> none  [paired_sums(): jnp.sum(residual * image)]
  transfers between devices with their start and end apart: 13 -> 0, of which waited for: 10 -> 0; matrix products, arithmetic and copies ran while one was open for 0% -> 0% of each run, Pallas kernels for 0% -> 0%
where the time goes in v1:
time: 49.2 us; the launch traced here: 49.1 us
  Pallas kernels  45.3 us (92%)
  local copies, waits for them, and re-layouts  3.81 us (8%)
    pallas_call x1, Pallas kernels, local(): pl.pallas_call(body, out_shape=jax.ShapeDtypeStruct((planes, rows, lanes)...  45.3 us
    unnamed x5, local copies, waits for them, and re-layouts  3.81 us

profile of v1, /device:TPU:0, one launch (start us, length us, event | category | flops | bytes accessed | tf_op | source)
XLA Modules:
  0.0 49.1 jit_solution(5066404680404030978)
XLA Ops:
  0.0 0.0 copy-start
  0.0 2.5 %copy-done = bf16[8,64,40,128]{3,2,1,0:T(8,128)(2,1)S(1)} copy-done((bf16[8,64,40,128]{3,2,1,0:T(8,128)(2,1)S(1)}, bf16[8,64,40,128]{3,2,1,0:T(8,128)(2,1)}, u32[]{:S(2)}) %copy-start) | copy-done | bytes 5242904
  2.5 0.0 copy-start.1
  2.5 0.7 %copy-done.1 = f32[8]{0:T(128)S(1)} copy-done((f32[8]{0:T(128)S(1)}, f32[8]{0:T(128)}, u32[]{:S(2)}) %copy-start.1) | copy-done | bytes 56
  3.1 45.3 %shard_map.28 = f32[8,40,128]{2,1,0:T(8,128)S(1)} custom-call(f32[8]{0:T(128)S(1)} %copy-done.1, bf16[8,64,40,128]{3,2,1,0:T(8,128)(2,1)S(1)} %copy-done), custom_call_target="tpu_custom_call" | custom-call | tf_op jit(solution)/shard_map/pallas_call | solution.py:282
  48.4 0.7 %copy.4 = f32[8,40,128]{2,1,0:T(8,128)} copy(f32[8,40,128]{2,1,0:T(8,128)S(1)} %shard_map.28) | data formatting | bytes 327680
Async XLA Ops:
  0.0 2.5 %copy-start = (bf16[8,64,40,128]{3,2,1,0:T(8,128)(2,1)S(1)}, bf16[8,64,40,128]{3,2,1,0:T(8,128)(2,1)}, u32[]{:S(2)}) copy-start(bf16[8,64,40,128]{3,2,1,0:T(8,128)(2,1)} %orb_ref.1) | copy-start | bytes 15728644
  2.5 0.7 %copy-start.1 = (f32[8]{0:T(128)S(1)}, f32[8]{0:T(128)}, u32[]{:S(2)}) copy-start(f32[8]{0:T(128)} %occ_ref.1) | copy-start | bytes 100

commit v2 on v1

--- a/solution.py
+++ b/solution.py
@@ -33,8 +33,8 @@
 
 
 def kernel(bands, spaces, groups, bands_total, chunks, orders, occ_ref, orb_ref, out_ref,
-           held, acc, got, field, first, second, mine, theirs, band_sum, space_sums,
-           load_sem, rs_send, rs_recv, halo_send, halo_recv, mb_send, mb_recv, ms_send, ms_recv):
+           held, acc, got, field, first, second, mine, theirs,
+           load_sem, rs_send, rs_recv, halo_send, halo_recv, mb_send, mb_recv, ready):
     b, s = lax.axis_index("band"), lax.axis_index("space")
     stages = len(orders[0])
     planes, rows, lanes = out_ref.shape
@@ -51,10 +51,9 @@
     field[...] = jnp.zeros_like(field)
 
     barrier = pltpu.get_barrier_semaphore()
-    greet = [((b + k) % bands, s) for k in range(1, bands)]
-    greet += [(b, (s + k) % spaces) for k in range(1, spaces)]
-    greet += [((b + db + bands) % bands, (s + ds + spaces) % spaces)
-              for db, ds in DIRECTIONS if db and ds]
+    greet = [(b + (1 << k) * (1 - 2 * ((b // (1 << k)) % 2)), s) for k in range(stages)]
+    across = [(b, (s + k) % spaces) for k in range(1, spaces)]
+    greet += across
     for peer in greet:
         pl.semaphore_signal(barrier, inc=1, device_id=peer, device_id_type=MESH)
 
@@ -95,7 +94,7 @@
         density(c, 0, bands // 2)
 
     scale = 4.0 * math.pi / bands_total
-    order = sorted(hops, key=lambda ct: (ct[0] // 2 + ct[1], -ct[1], ct[0]))
+    order = sorted(hops, key=lambda ct: (ct[1], ct[0]))
     for c, t in order:
         half = bands >> (t + 1)
         hops[c, t].wait_recv()
@@ -111,6 +110,9 @@
             hops[c, t + 1].start()
             lax.fori_loop(0, quarter * part, add, 0)
         else:
+            if c == 0:
+                for peer in across:
+                    pl.semaphore_signal(ready, inc=1, device_id=peer, device_id_type=MESH)
             for plane in range(part):
                 field[DEEP + c * part + plane, EDGE:EDGE + rows] = scale * (
                     acc[c, 0, plane] + got[c, 1, plane])
@@ -120,9 +122,10 @@
             return size + halo - width, halo - width
         return halo, size + halo
 
+    pl.semaphore_wait(ready, len(across))
     halos = []
     for i, (db, ds) in enumerate(DIRECTIONS):
-        deep = DEEP if not ds else (CORNER if db else planes)
+        deep = planes if not db else (DEEP if (db, ds) == (-1, 0) else CORNER)
         wide = EDGE if ds else rows
         src_p, dst_p = span(db, planes, deep, DEEP) if db else (DEEP, DEEP)
         src_r, dst_r = span(ds, rows, wide, EDGE) if ds else (EDGE, EDGE)
@@ -164,10 +167,14 @@
     low_plane = jnp.where(b == 0, DEEP, 0)
     high_plane = jnp.where(b == bands - 1, DEEP + planes, planes + 2 * DEEP)
 
-    def apply(ref, p):
+    def apply(ref, p, forward=False):
         v = ref[p]
-        ones = ref[p - 1] + ref[p + 1] + pltpu.roll(v, 1, 0) + pltpu.roll(v, tall - 1, 0)
-        twos = ref[p - 2] + ref[p + 2] + pltpu.roll(v, 2, 0) + pltpu.roll(v, tall - 2, 0)
+        if forward:
+            ones, twos = 2.0 * ref[p + 1], 2.0 * ref[p + 2]
+        else:
+            ones, twos = ref[p - 1] + ref[p + 1], ref[p - 2] + ref[p + 2]
+        ones = ones + pltpu.roll(v, 1, 0) + pltpu.roll(v, tall - 1, 0)
+        twos = twos + pltpu.roll(v, 2, 0) + pltpu.roll(v, tall - 2, 0)
         total = 7.5 * v + near * ones + far * twos
         for shift, coefficient in lane_terms:
             total = total + coefficient * pltpu.roll(v, shift, 1)
@@ -180,8 +187,8 @@
             return 0
         return body
 
-    lax.fori_loop(REACH, planes + 2 * DEEP - REACH, step(field, first), 0)
-    lax.fori_loop(2 * REACH, planes + 2 * DEEP - 2 * REACH, step(first, second), 0)
+    lax.fori_loop(2 * REACH, planes + 2 * DEEP - REACH, step(field, first), 0)
+    lax.fori_loop(DEEP, planes + 2 * DEEP - 2 * REACH, step(first, second), 0)
 
     def fold(x):
         x = x[EDGE:EDGE + rows]
@@ -192,42 +199,31 @@
 
     def moments(p, sums):
         w0, w1, w2 = field[p], first[p], second[p]
-        w3 = apply(second, p)
+        w3 = apply(second, p, forward=True)
         terms = (w0 * w0, w0 * w1, w1 * w1, w1 * w2, w2 * w2, w2 * w3)
         return tuple(x + fold(y) for x, y in zip(sums, terms))
 
     sums = lax.fori_loop(DEEP, DEEP + planes, moments,
                          tuple(jnp.zeros((8, lanes), jnp.float32) for _ in range(6)))
-    packed = [jnp.sum(x, axis=0, keepdims=True) for x in sums]
-    packed = jnp.concatenate(packed + [jnp.zeros((2, lanes), jnp.float32)], axis=0)
+    slot = lax.broadcasted_iota(jnp.int32, (1, lanes), 1)
+    packed = jnp.zeros((1, lanes), jnp.float32)
+    for k, x in enumerate(sums):
+        value = jnp.sum(jnp.sum(x, axis=0, keepdims=True), axis=1, keepdims=True)
+        packed = packed + jnp.where(slot == k, value, 0.0)
     mine[...] = packed
+    me = b * spaces + s
     copies = []
-    for k in range(1, bands):
+    for k in range(bands * spaces - 1, 0, -1):
+        to = ((b + k // spaces) % bands, (s + k % spaces) % spaces)
         copies.append(pltpu.make_async_remote_copy(
-            src_ref=mine, dst_ref=theirs.at[b], send_sem=mb_send.at[k], recv_sem=mb_recv.at[k],
-            device_id=((b + k) % bands, s), device_id_type=MESH))
+            src_ref=mine, dst_ref=theirs.at[me], send_sem=mb_send.at[k], recv_sem=mb_recv.at[k],
+            device_id=to, device_id_type=MESH))
         copies[-1].start()
-    theirs[b] = packed
+    theirs[me] = packed
     for copy in copies:
         copy.wait_recv()
-    total = theirs[0]
-    for k in range(1, bands):
-        total = total + theirs[k]
-    band_sum[...] = total
-    across = []
-    for k in range(1, spaces):
-        across.append(pltpu.make_async_remote_copy(
-            src_ref=band_sum, dst_ref=space_sums.at[s], send_sem=ms_send.at[k],
-            recv_sem=ms_recv.at[k], device_id=(b, (s + k) % spaces), device_id_type=MESH))
-        across[-1].start()
-    space_sums[s] = total
-    for copy in across:
-        copy.wait_recv()
-    total = space_sums[0]
-    for k in range(1, spaces):
-        total = total + space_sums[k]
-    total = jnp.sum(total, axis=1, keepdims=True)
-    mu = [total[k:k + 1] for k in range(6)]
+    total = jnp.sum(theirs[...], axis=0)
+    mu = [jnp.sum(jnp.where(slot == k, total, 0.0), axis=1, keepdims=True) for k in range(6)]
 
     def form(c, shift):
         value = None
@@ -259,7 +255,7 @@
 
     for c, t in order:
         hops[c, t].wait_send()
-    for copy in copies + across:
+    for copy in copies:
         copy.wait_send()
 
 
@@ -282,7 +278,7 @@
         return pl.pallas_call(
             body,
             out_shape=jax.ShapeDtypeStruct((planes, rows, lanes), f32),
-            in_specs=[pl.BlockSpec(memory_space=pltpu.SMEM), pl.BlockSpec(memory_space=pl.ANY)],
+            in_specs=[pl.BlockSpec(memory_space=pltpu.SMEM), pl.BlockSpec(memory_space=pltpu.HBM)],
             out_specs=pl.BlockSpec(memory_space=pltpu.VMEM),
             scratch_shapes=[
                 pltpu.VMEM((bands, groups, planes, rows, lanes), orbitals.dtype),
@@ -291,22 +287,19 @@
                 pltpu.VMEM((deep, tall, lanes), f32),
                 pltpu.VMEM((deep, tall, lanes), f32),
                 pltpu.VMEM((deep, tall, lanes), f32),
-                pltpu.VMEM((8, lanes), f32),
-                pltpu.VMEM((bands, 8, lanes), f32),
-                pltpu.VMEM((8, lanes), f32),
-                pltpu.VMEM((spaces, 8, lanes), f32),
+                pltpu.VMEM((1, lanes), f32),
+                pltpu.VMEM((bands * spaces, 1, lanes), f32),
                 pltpu.SemaphoreType.DMA((bands,)),
                 pltpu.SemaphoreType.DMA((chunks, stages)),
                 pltpu.SemaphoreType.DMA((chunks, stages)),
                 pltpu.SemaphoreType.DMA((len(DIRECTIONS),)),
                 pltpu.SemaphoreType.DMA((len(DIRECTIONS),)),
-                pltpu.SemaphoreType.DMA((bands,)),
-                pltpu.SemaphoreType.DMA((bands,)),
-                pltpu.SemaphoreType.DMA((spaces,)),
-                pltpu.SemaphoreType.DMA((spaces,)),
+                pltpu.SemaphoreType.DMA((bands * spaces,)),
+                pltpu.SemaphoreType.DMA((bands * spaces,)),
+                pltpu.SemaphoreType.REGULAR,
             ],
             compiler_params=pltpu.CompilerParams(
-                collective_id=0, has_side_effects=True, vmem_limit_bytes=48 * 1024 * 1024),
+                collective_id=0, has_side_effects=True, vmem_limit_bytes=67043328),
         )(occupations, orbitals)
 
     in_specs = (P("band", None, "space", None), P("band"))

time: 49.2 us -> 42.3 us (0.86)
  Pallas kernels: 45.3 us -> 40.6 us
  local copies, waits for them, and re-layouts: 3.81 us -> 1.59 us
    pallas_call x1, Pallas kernels: 45.3 us -> 40.6 us  [local(): pl.pallas_call(body, out_shape=jax.ShapeDtypeStruct((planes, rows, lanes)...]
    unnamed x5 -> x1, local copies, waits for them, and re-layouts: 3.81 us -> 1.59 us
where the time goes in v2:
time: 42.3 us; the launch traced here: 42.2 us
  Pallas kernels  40.6 us (96%)
  local copies, waits for them, and re-layouts  1.59 us (4%)
    pallas_call x1, Pallas kernels, local(): pl.pallas_call(body, out_shape=jax.ShapeDtypeStruct((planes, rows, lanes)...  40.6 us
    unnamed x1, local copies, waits for them, and re-layouts  1.59 us

profile of v2, /device:TPU:0, one launch (start us, length us, event | category | flops | bytes accessed | tf_op | source)
XLA Modules:
  0.0 42.2 jit_solution(11050767934593133566)
XLA Ops:
  0.0 40.6 %shard_map.28 = f32[8,40,128]{2,1,0:T(8,128)} custom-call(f32[8]{0:T(128)} %occ_ref.1, bf16[8,64,40,128]{3,2,1,0:T(8,128)(2,1)} %orb_ref.1), custom_call_target="tpu_custom_call" | custom-call | tf_op jit(solution)/shard_map/pallas_call | solution.py:278
  40.6 1.6 %copy.4 = f32[8,40,128]{2,1,0:T(8,128)} copy(f32[8,40,128]{2,1,0:T(8,128)} %shard_map.28) | data formatting | bytes 327680
